TPU v7x, 256 devices: a whole 4x4x8 slice. The times are simulated.
256 devices in a mesh: ka: 32 (over z_hi, x, y), ga: 8 (over z_lo, core).
Axes of the slice: x: 4, y: 4, z: 8 (z_hi: 2, z_lo: 4; z = z_hi * 4 + z_lo), core: 2. Of those that a mesh axis runs over, the one named last changes fastest.
Arguments:
- psi: bfloat16 [32, 2, 128, 2048], P('ka', None, None, 'ga'), may hold values from -0.62890625 to 0.62890625
- dvscf: bfloat16 [96, 2, 2048], P(None, None, 'ga'), may hold values from -6 to 6
- kq_map: int32 [32], P('ka'), may hold values from 0 to 31, each once
Outputs:
- coupling: float32 [96, 32, 2, 128, 128], P('ga', 'ka')
Inputs may be any that keep to these rules, and one draw needn't show every extreme that they name: kq_map is a permutation of the k-points 0 to 31.
All inputs are finite; a program needn't handle non-finite values.
Results may differ from a plain program's by a relative error of at most 0.0029.
Values may be sent and summed in bfloat16 or wider, within the bound.
No kernel may reach another device: no remote copies, remote signals or barrier semaphores. Data moves between devices by JAX's collectives and lax.ppermute only.
A program may use at most 128 MiB of HBM per device.

v0:
```python
import jax
import jax.numpy as jnp
from jax import lax
from jax.sharding import Mesh
from jax.sharding import PartitionSpec as P

KA = ("ka_0", "ka_1", "ka_2")


def joined_along(blocks, dim):
    dims = list(blocks.shape[1:])
    dims[dim] *= blocks.shape[0]
    return jnp.moveaxis(blocks, 0, dim).reshape(dims)


def gather_in_order(value, axes, sequence):
    blocks = value[None]
    for k in sequence:
        blocks = lax.all_gather(blocks, axes[k], axis=0, tiled=True)
    current = [lax.axis_size(axes[k]) for k in reversed(sequence)]
    blocks = blocks.reshape(*current, *value.shape)
    turned = sorted(range(len(sequence)), key=lambda place: sequence[len(sequence) - 1 - place])
    return blocks.transpose(*turned, *range(len(sequence), blocks.ndim)).reshape(-1, *value.shape)


def gathered_by_axis(value, axes, sequence, dim):
    return joined_along(gather_in_order(value, axes, sequence), dim)


def in_one_piece(arrays, axis, dim, along):
    ends, at = ([], 0)
    for a in arrays[:-1]:
        at += a.shape[along]
        ends.append(at)
    both = jnp.concatenate(arrays, axis=along)
    return tuple(jnp.split(lax.all_gather(both, axis, axis=dim, tiled=True), ends, axis=along))


def block_modes(left, wave_real, wave_imag, potential):
    dv_real = potential[:, 0].astype(jnp.float32)[:, None, None, :]
    dv_imag = potential[:, 1].astype(jnp.float32)[:, None, None, :]
    prod_real = (dv_real * wave_real[None] - dv_imag * wave_imag[None]).astype(jnp.bfloat16)
    prod_imag = (dv_real * wave_imag[None] + dv_imag * wave_real[None]).astype(jnp.bfloat16)
    right = jnp.stack(
        [
            jnp.concatenate([prod_real, prod_imag], axis=-1),
            jnp.concatenate([prod_imag, -prod_real], axis=-1),
        ],
        axis=2,
    )
    return jnp.einsum("kmr,ukcnr->ukcmn", left, right, preferred_element_type=jnp.float32)


def mode_block(left, wave, dv_block):
    wave_real = wave[:, 0].astype(jnp.float32)
    wave_imag = wave[:, 1].astype(jnp.float32)
    return block_modes(left, wave_real, wave_imag, dv_block)


def stack_left(other):
    return jnp.concatenate([other[:, 0], other[:, 1]], axis=-1)


def body(psi, dvscf, kq_map):
    piece = gathered_by_axis(psi, KA, (0, 1, 2), 0)
    within = (kq_map >= 0) & (kq_map < piece.shape[0])
    clipped = jnp.clip(kq_map, 0, piece.shape[0] - 1)
    taken = jnp.take(piece, clipped, axis=0)
    phi = jnp.where(within[:, None, None, None], taken, jnp.zeros_like(psi))
    dv_modes = lax.all_to_all(dvscf, "ga", split_axis=0, concat_axis=2, tiled=True)
    wave_piece, other_piece = in_one_piece((psi, phi), "ga", 3, 0)
    return mode_block(stack_left(other_piece), wave_piece, dv_modes)


def solution(mesh):
    finer = Mesh(mesh.devices.reshape(2, 4, 4, mesh.shape["ga"]), ("ka_0", "ka_1", "ka_2", "ga"))
    in_specs = (P(KA, None, None, "ga"), P(None, None, "ga"), P(KA))
    out_specs = P("ga", KA, None, None, None)
    return jax.shard_map(body, mesh=finer, in_specs=in_specs, out_specs=out_specs, check_vma=False)
```

profile of v0, /device:TPU:1, one launch (start us, length us, event | category | flops | bytes accessed | tf_op | source)
XLA Modules:
  0.0 180.3 jit_solution(7627843267096762044)
XLA Ops:
  6.5 0.0 all-gather.9.cloned.1.call-start
  6.5 13.4 %all-gather = bf16[2,2,128,256]{3,2,1,0:T(8,128)(2,1)} all-gather(bf16[1,2,128,256]{3,2,1,0:T(8,128)(2,1)} %param.3), channel_id=2, replica_groups=mesh['ka_0'=2,'ka_1'=4,'ka_2'=4,'ga'=8] {'ka_0'}, dimensions={0}, use_global_device_ids=true | all-gather | bytes 393216 | tf_op jit(solution)/shard_map/all_gather | solution.py:19
  19.9 0.0 all-gather.9.cloned.1.call-update
  19.9 0.0 all-gather.11.cloned.1.call-start
  20.0 27.5 %all-gather.9.cloned.1.call-done = bf16[8,2,128,256]{3,2,1,0:T(8,128)(2,1)} async-done(((bf16[2,2,128,256]{3,2,1,0:T(8,128)(2,1)}), bf16[8,2,128,256]{3,2,1,0:T(8,128)(2,1)}) %all-gather.9.cloned.1.call-update) | async-done | bytes 1048592 | tf_op jit(solution)/shard_map/all_gather | solution.py:19
  47.5 0.0 all-gather.11.cloned.1.call-update
  47.6 0.0 all-gather.7.cloned.1.call-start
  48.3 54.2 %all-gather.11.cloned.1.call-done = bf16[32,2,128,256]{3,2,1,0:T(8,128)(2,1)} async-done(((bf16[8,2,128,256]{3,2,1,0:T(8,128)(2,1)}), bf16[32,2,128,256]{3,2,1,0:T(8,128)(2,1)}) %all-gather.11.cloned.1.call-update) | async-done | bytes 4194320 | tf_op jit(solution)/shard_map/all_gather | solution.py:19
  102.5 2.5 %copy.13 = bf16[4,4,2,1,2,128,256]{6,5,4,0,1,2,3:T(8,128)(2,1)S(1)} copy(bf16[4,4,2,1,2,128,256]{6,5,4,2,1,0,3:T(8,128)(2,1)} %bitcast.54) | data formatting | bytes 8388608 | tf_op jit(solution)/shard_map/reshape | solution.py:21
  104.9 1.6 pad_maximum_fusion
  106.6 0.0 all-gather.7.cloned.1.call-update
  106.6 11.0 %all_to_all.18 = bf16[96,2,256]{2,1,0:T(2,128)(2,1)S(1)} all-to-all(bf16[96,2,256]{2,1,0:T(2,128)(2,1)} %param.4), channel_id=1, replica_groups=mesh['ka_0'=2,'ka_1'=4,'ka_2'=4,'ga'=8] {'ga'}, dimensions={0} | all-to-all | bytes 196608 | tf_op jit(solution)/shard_map/all_to_all | solution.py:70
  117.7 0.1 slice_convert_fusion.1
  117.8 0.1 copy_bitcast_fusion
  117.9 28.4 %all-gather.7.cloned.1.call-done = bf16[2,2,128,2048]{3,2,1,0:T(8,128)(2,1)} async-done(((bf16[2,2,128,256]{3,2,1,0:T(8,128)(2,1)}), bf16[2,2,128,2048]{3,2,1,0:T(8,128)(2,1)}) %all-gather.7.cloned.1.call-update) | async-done | bytes 2097168 | tf_op jit(solution)/shard_map/all_gather | solution.py:36
  146.3 2.8 %slice_bitcast_fusion.1 = (bf16[1,128,2048]{2,1,0:T(8,128)(2,1)}, bf16[1,128,2048]{2,1,0:T(8,128)(2,1)}, f32[128,2048]{1,0:T(8,128)S(1)}, f32[128,2048]{1,0:T(8,128)S(1)}) fusion(bf16[2,2,128,2048]{3,2,1,0:T(8,128)(2,1)} %all-gather.7.cloned.1.call-done), kind=kLoop, calls=%fused_computation.13 | loop fusion | flops 524288 | bytes 5242880 | tf_op jit(solution)/shard_map/squeeze | solution.py:61
  149.1 1.9 %fusion.10 = bf16[12,1,128,2048]{3,2,0,1:T(8,128)(2,1)S(1)} fusion(f32[128,2048]{1,0:T(8,128)S(1)} %get-tuple-element.22, f32[12,2048]{1,0:T(8,128)S(1)} %get-tuple-element.26, f32[128,2048]{1,0:T(8,128)S(1)} %get-tuple-element.23, f32[12,2048]{1,0:T(8,128)S(1)} %get-tuple-element.27), kind=kLoop, calls=%fused_computation.27 | loop fusion | flops 15728640 | bytes 8585216 | tf_op jit(solution)/shard_map/neg | solution.py:47
  151.0 3.4 %subtract_convert_fusion = (bf16[12,1,128,2048]{3,2,0,1:T(8,128)(2,1)S(1)}, bf16[12,1,128,2048]{3,2,0,1:T(8,128)(2,1)S(1)}) fusion(f32[128,2048]{1,0:T(8,128)S(1)} %get-tuple-element.22, f32[12,2048]{1,0:T(8,128)S(1)} %get-tuple-element.26, f32[128,2048]{1,0:T(8,128)S(1)} %get-tuple-element.23, f32[12,2048]{1,0:T(8,128)S(1)} %get-tuple-element.27), kind=kLoop, calls=%fused_computation.7 | loop fusion | flops 25165824 | bytes 14876672 | tf_op jit(solution)/shard_map/convert_element_type | solution.py:42
  154.4 5.5 %maximum_bitcast_fusion.2 = (bf16[12,1,1,128,4096]{4,3,2,0,1:T(8,128)(2,1)S(1)}, bf16[12,1,1,128,4096]{4,3,2,0,1:T(8,128)(2,1)}) fusion(bf16[12,1,128,2048]{3,2,0,1:T(8,128)(2,1)S(1)} %get-tuple-element.19, bf16[12,1,128,2048]{3,2,0,1:T(8,128)(2,1)S(1)} %get-tuple-element.18, bf16[12,1,128,2048]{3,2,0,1:T(8,128)(2,1)S(1)} %fusion.10), kind=kLoop, calls=%fused_computation.4 | loop fusion | flops 50331648 | bytes 44040192 | tf_op jit(solution)/shard_map/stack | solution.py:44
  159.9 10.8 %fusion.3 = f32[12,1,2,128,128]{3,4,2,0,1:T(8,128)} fusion(bf16[12,1,1,128,4096]{4,3,2,0,1:T(8,128)(2,1)} %get-tuple-element.17, bf16[12,1,1,128,4096]{4,3,2,0,1:T(8,128)(2,1)S(1)} %get-tuple-element.16, bf16[1,128,2048]{2,1,0:T(8,128)(2,1)} %get-tuple-element.21, bf16[1,128,2048]{2,1,0:T(8,128)(2,1)} %get-tuple-element.20), kind=kOutput, calls=%fused_computation.8 | convolution fusion | flops 3235905536 | bytes 27787264 | tf_op jit(solution)/shard_map/kmr,ukcnr->ukcmn/dot_general | solution.py:51
  170.7 3.0 %copy.15 = f32[12,1,2,128,128]{4,3,2,1,0:T(8,128)} copy(f32[12,1,2,128,128]{3,4,2,0,1:T(8,128)} %fusion.3) | data formatting | bytes 3145728 | tf_op jit(solution)/shard_map/kmr,ukcnr->ukcmn/transpose | solution.py:51
  (3 shorter events, 0.1 us)
Async XLA Ops:
  6.5 41.0 %all-gather.9.cloned.1.call-start = ((), (), s32[]{:S(2)}) async-start(), calls=%async_computation.2 | async-start | bytes 1310720 | tf_op jit(solution)/shard_map/all_gather | solution.py:19
  19.9 82.5 %all-gather.11.cloned.1.call-start = ((), (), s32[]{:S(2)}) async-start(), calls=%async_computation.3 | async-start | bytes 5242880 | tf_op jit(solution)/shard_map/all_gather | solution.py:19
  47.6 98.7 %all-gather.7.cloned.1.call-start = ((), (), s32[]{:S(2)}) async-start(), calls=%async_computation.1 | async-start | bytes 2359296 | tf_op jit(solution)/shard_map/all_gather | solution.py:36
Sparse Core Ops, SparseCore 0:
  20.1 27.4 all-gather.8
  49.3 53.0 all-gather.10
  106.7 39.5 all-gather.6
where the time goes:
time: 181 us; the launch traced here: 180 us
  waiting for transfers between devices  110 us (61%)
  blocking collectives  24.4 us (13%)
  other arithmetic  15.4 us (9%)
  between operations  13.8 us (8%)
  matrix products  10.8 us (6%)
  local copies, waits for them, and re-layouts  5.59 us (3%)
    all_gather x2, waiting for transfers between devices, gather_in_order(): blocks = lax.all_gather(blocks, axes[k], axis=0, tiled=True)  81.7 us
    all_gather x1, waiting for transfers between devices, in_one_piece(): lax.all_gather(both, axis, axis=dim, tiled=True)  28.4 us
    all_gather x1, blocking collectives, gather_in_order(): blocks = lax.all_gather(blocks, axes[k], axis=0, tiled=True)  13.4 us
    all_to_all x1, blocking collectives, body(): lax.all_to_all(dvscf, 'ga', split_axis=0, concat_axis=2, tiled=True)  11 us
    dot_general x1, matrix products, block_modes(): jnp.einsum('kmr,ukcnr->ukcmn', left, right, preferred_element_type=jnp.fl...  10.8 us
    another operation x1, other arithmetic, block_modes(): jnp.stack([jnp.concatenate([prod_real, prod_imag], axis=-1), jnp.concaten...  5.48 us
  transfers between devices with their start and end apart: 3, of which 3 were waited for; matrix products, arithmetic and copies ran while one was open for 0% of the time, Pallas kernels for 0%

commit v1 on v0

--- a/solution.py
+++ b/solution.py
@@ -16,7 +16,9 @@
 def gather_in_order(value, axes, sequence):
     blocks = value[None]
     for k in sequence:
-        blocks = lax.all_gather(blocks, axes[k], axis=0, tiled=True)
+        blocks = jnp.concatenate(
+            lax.all_to_all(jnp.stack([blocks] * lax.axis_size(axes[k])), axes[k], 0, 0), axis=0
+        )
     current = [lax.axis_size(axes[k]) for k in reversed(sequence)]
     blocks = blocks.reshape(*current, *value.shape)
     turned = sorted(range(len(sequence)), key=lambda place: sequence[len(sequence) - 1 - place])

time: 181 us -> 174 us (0.961)
  waiting for transfers between devices: 110 us -> 67 us
  blocking collectives: 24.4 us -> 52.1 us
  starting transfers between devices: 0.08 us -> 4.88 us
  other arithmetic: 15.4 us -> 17.6 us
    all_gather x2 -> x0, waiting for transfers between devices: 81.7 us -> none  [gather_in_order(): blocks = lax.all_gather(blocks, axes[k], axis=0, tiled=True)]
    all_to_all x0 -> x1, waiting for transfers between devices: none -> 42.9 us  [gather_in_order(): lax.all_to_all(jnp.stack([blocks] * lax.axis_size(axes[k])), axes[k], 0, 0)]
    all_to_all x0 -> x2, blocking collectives: none -> 31.5 us  [gather_in_order(): lax.all_to_all(jnp.stack([blocks] * lax.axis_size(axes[k])), axes[k], 0, 0)]
    all_gather x1 -> x0, blocking collectives: 13.4 us -> none  [gather_in_order(): blocks = lax.all_gather(blocks, axes[k], axis=0, tiled=True)]
    all_to_all x1, blocking collectives: 11 us -> 20.7 us  [body(): lax.all_to_all(dvscf, 'ga', split_axis=0, concat_axis=2, tiled=True)]
    all_to_all x0 -> x1, starting transfers between devices: none -> 4.84 us  [gather_in_order(): lax.all_to_all(jnp.stack([blocks] * lax.axis_size(axes[k])), axes[k], 0, 0)]
    all_gather x1, waiting for transfers between devices: 28.4 us -> 24 us  [in_one_piece(): lax.all_gather(both, axis, axis=dim, tiled=True)]
    another operation x1, other arithmetic: 5.48 us -> 8.68 us  [block_modes(): jnp.stack([jnp.concatenate([prod_real, prod_imag], axis=-1), jnp.concaten...]
  transfers between devices with their start and end apart: 3 -> 2, of which waited for: 3 -> 2; matrix products, arithmetic and copies ran while one was open for 0% -> 0% of each run, Pallas kernels for 0% -> 0%
where the time goes in v1:
time: 174 us
  waiting for transfers between devices  67 us (39%)
  blocking collectives  52.1 us (30%)
  other arithmetic  17.6 us (10%)
  between operations  14.2 us (8%)
  matrix products  11.4 us (7%)
  local copies, waits for them, and re-layouts  6.77 us (4%)
  starting transfers between devices  4.88 us (3%)
    all_to_all x1, waiting for transfers between devices, gather_in_order(): lax.all_to_all(jnp.stack([blocks] * lax.axis_size(axes[k])), axes[k], 0, 0)  42.9 us
    all_to_all x2, blocking collectives, gather_in_order(): lax.all_to_all(jnp.stack([blocks] * lax.axis_size(axes[k])), axes[k], 0, 0)  31.5 us
    all_gather x1, waiting for transfers between devices, in_one_piece(): lax.all_gather(both, axis, axis=dim, tiled=True)  24 us
    all_to_all x1, blocking collectives, body(): lax.all_to_all(dvscf, 'ga', split_axis=0, concat_axis=2, tiled=True)  20.7 us
    dot_general x1, matrix products, block_modes(): jnp.einsum('kmr,ukcnr->ukcmn', left, right, preferred_element_type=jnp.fl...  11.4 us
    another operation x1, other arithmetic, block_modes(): jnp.stack([jnp.concatenate([prod_real, prod_imag], axis=-1), jnp.concaten...  8.68 us
    all_to_all x1, starting transfers between devices, gather_in_order(): lax.all_to_all(jnp.stack([blocks] * lax.axis_size(axes[k])), axes[k], 0, 0)  4.84 us
  transfers between devices with their start and end apart: 2, of which 2 were waited for; matrix products, arithmetic and copies ran while one was open for 0% of the time, Pallas kernels for 0%

profile of v1, /device:TPU:1, one launch (start us, length us, event | category | flops | bytes accessed | tf_op | source)
XLA Modules:
  0.0 174.0 jit_solution(8999547074585566875)
XLA Ops:
  6.5 1.0 pad_maximum_fusion
  7.5 16.8 %all_to_all.33 = bf16[2,1,1,2,128,256]{5,4,3,2,1,0:T(8,128)(2,1)S(1)} all-to-all(bf16[2,1,1,2,128,256]{5,4,3,2,1,0:T(8,128)(2,1)S(1)} %pad_maximum_fusion), channel_id=1, replica_groups=mesh['ka_0'=2,'ka_1'=4,'ka_2'=4,'ga'=8] {'ka_0'}, dimensions={0} | all-to-all | bytes 524288 | tf_op jit(solution)/shard_map/all_to_all | solution.py:20
  24.4 0.0 copy-start
  24.4 0.1 stack.19
  24.5 0.0 copy-start.1
  24.5 14.7 %all_to_all.34 = bf16[4,2,1,2,128,256]{5,4,3,1,2,0:T(8,128)(2,1)S(1)} all-to-all(bf16[4,2,1,2,128,256]{5,4,3,1,2,0:T(8,128)(2,1)S(1)} %stack.19), channel_id=1, replica_groups=mesh['ka_0'=2,'ka_1'=4,'ka_2'=4,'ga'=8] {'ka_1'}, dimensions={0} | all-to-all | bytes 2097152 | tf_op jit(solution)/shard_map/all_to_all | solution.py:20
  39.1 2.5 %stack.20 = bf16[4,8,1,2,128,256]{5,4,3,1,2,0:T(8,128)(2,1)} broadcast(bf16[8,2,128,256]{3,2,1,0:T(8,128)(2,1)S(1)} %bitcast.57), dimensions={1,3,4,5} | broadcast | bytes 5242880 | tf_op jit(solution)/shard_map/stack | solution.py:20
  41.6 4.8 %all-to-all-start.3 = ((bf16[4,8,1,2,128,256]{5,4,3,1,2,0:T(8,128)(2,1)}), bf16[4,8,1,2,128,256]{5,4,3,1,2,0:T(8,128)(2,1)}, u32[]{:S(2)}, u32[]{:S(2)}) async-start(bf16[4,8,1,2,128,256]{5,4,3,1,2,0:T(8,128)(2,1)} %stack.20), calls=%async_computation.3 | async-start | bytes 8388608 | tf_op jit(solution)/shard_map/all_to_all | solution.py:20
  46.5 0.0 all-gather.2.cloned.1.call-start
  47.2 42.9 %all-to-all-done.3 = bf16[4,8,1,2,128,256]{5,4,3,1,2,0:T(8,128)(2,1)} async-done(((bf16[4,8,1,2,128,256]{5,4,3,1,2,0:T(8,128)(2,1)}), bf16[4,8,1,2,128,256]{5,4,3,1,2,0:T(8,128)(2,1)}, u32[]{:S(2)}, u32[]{:S(2)}) %all-to-all-start.3) | async-done | bytes 4194336 | tf_op jit(solution)/shard_map/all_to_all | solution.py:20
  90.1 2.5 %copy.12 = bf16[2,4,4,1,2,128,256]{6,5,4,2,1,0,3:T(8,128)(2,1)S(1)} copy(bf16[2,4,4,1,2,128,256]{6,5,4,0,1,2,3:T(8,128)(2,1)} %bitcast.8) | data formatting | bytes 8388608 | tf_op jit(solution)/shard_map/transpose | solution.py:25
  92.6 0.0 copy-done
  92.6 0.7 pad_maximum_fusion.1
  93.3 0.0 all-gather.2.cloned.1.call-update
  93.3 0.0 copy-done.1
  93.3 20.7 %all_to_all.35 = bf16[96,2,256]{2,1,0:T(2,128)(2,1)S(1)} all-to-all(bf16[96,2,256]{2,1,0:T(2,128)(2,1)S(1)} %copy-done.1), channel_id=1, replica_groups=mesh['ka_0'=2,'ka_1'=4,'ka_2'=4,'ga'=8] {'ga'}, dimensions={0} | all-to-all | bytes 196608 | tf_op jit(solution)/shard_map/all_to_all | solution.py:72
  114.1 0.1 slice_convert_fusion.1
  114.2 0.1 copy_bitcast_fusion
  114.3 24.0 %all-gather.2.cloned.1.call-done = bf16[2,2,128,2048]{3,2,1,0:T(8,128)(2,1)} async-done(((bf16[2,2,128,256]{3,2,1,0:T(8,128)(2,1)}), bf16[2,2,128,2048]{3,2,1,0:T(8,128)(2,1)}) %all-gather.2.cloned.1.call-update) | async-done | bytes 2097168 | tf_op jit(solution)/shard_map/all_gather | solution.py:38
  138.3 1.8 %slice_bitcast_fusion.1 = (bf16[1,128,2048]{2,1,0:T(8,128)(2,1)S(1)}, bf16[1,128,2048]{2,1,0:T(8,128)(2,1)S(1)}, f32[128,2048]{1,0:T(8,128)S(1)}, f32[128,2048]{1,0:T(8,128)S(1)}) fusion(bf16[2,2,128,2048]{3,2,1,0:T(8,128)(2,1)} %all-gather.2.cloned.1.call-done), kind=kLoop, calls=%fused_computation.13 | loop fusion | flops 524288 | bytes 5242880 | tf_op jit(solution)/shard_map/squeeze | solution.py:63
  140.1 2.0 %fusion.10 = bf16[12,1,128,2048]{3,2,0,1:T(8,128)(2,1)S(1)} fusion(f32[128,2048]{1,0:T(8,128)S(1)} %get-tuple-element.22, f32[12,2048]{1,0:T(8,128)S(1)} %get-tuple-element.26, f32[128,2048]{1,0:T(8,128)S(1)} %get-tuple-element.23, f32[12,2048]{1,0:T(8,128)S(1)} %get-tuple-element.27), kind=kLoop, calls=%fused_computation.28 | loop fusion | flops 15728640 | bytes 8585216 | tf_op jit(solution)/shard_map/neg | solution.py:49
  142.1 3.3 %subtract_convert_fusion = (bf16[12,1,128,2048]{3,2,0,1:T(8,128)(2,1)S(1)}, bf16[12,1,128,2048]{3,2,0,1:T(8,128)(2,1)S(1)}) fusion(f32[128,2048]{1,0:T(8,128)S(1)} %get-tuple-element.22, f32[12,2048]{1,0:T(8,128)S(1)} %get-tuple-element.26, f32[128,2048]{1,0:T(8,128)S(1)} %get-tuple-element.23, f32[12,2048]{1,0:T(8,128)S(1)} %get-tuple-element.27), kind=kLoop, calls=%fused_computation.7 | loop fusion | flops 25165824 | bytes 14876672 | tf_op jit(solution)/shard_map/convert_element_type | solution.py:44
  145.4 8.7 %maximum_bitcast_fusion.2 = (bf16[12,1,1,128,4096]{4,3,2,0,1:T(8,128)(2,1)}, bf16[12,1,1,128,4096]{4,3,2,0,1:T(8,128)(2,1)}) fusion(bf16[12,1,128,2048]{3,2,0,1:T(8,128)(2,1)S(1)} %get-tuple-element.19, bf16[12,1,128,2048]{3,2,0,1:T(8,128)(2,1)S(1)} %get-tuple-element.18, bf16[12,1,128,2048]{3,2,0,1:T(8,128)(2,1)S(1)} %fusion.10), kind=kLoop, calls=%fused_computation.4 | loop fusion | flops 50331648 | bytes 44040192 | tf_op jit(solution)/shard_map/stack | solution.py:46
  154.1 11.4 %fusion.3 = f32[12,1,2,128,128]{3,4,2,0,1:T(8,128)S(1)} fusion(bf16[12,1,1,128,4096]{4,3,2,0,1:T(8,128)(2,1)} %get-tuple-element.17, bf16[12,1,1,128,4096]{4,3,2,0,1:T(8,128)(2,1)} %get-tuple-element.16, bf16[1,128,2048]{2,1,0:T(8,128)(2,1)S(1)} %get-tuple-element.21, bf16[1,128,2048]{2,1,0:T(8,128)(2,1)S(1)} %get-tuple-element.20), kind=kOutput, calls=%fused_computation.8 | convolution fusion | flops 3235905536 | bytes 27787264 | tf_op jit(solution)/shard_map/kmr,ukcnr->ukcmn/dot_general | solution.py:53
  165.5 1.6 copy.14
  (3 shorter events, 0.1 us)
Async XLA Ops:
  24.4 68.2 %copy-start = (bf16[1,2,128,256]{3,2,1,0:T(8,128)(2,1)S(1)}, bf16[1,2,128,256]{3,2,1,0:T(8,128)(2,1)}, u32[]{:S(2)}) copy-start(bf16[1,2,128,256]{3,2,1,0:T(8,128)(2,1)} %param.3) | copy-start | bytes 393220
  24.5 68.9 %copy-start.1 = (bf16[96,2,256]{2,1,0:T(2,128)(2,1)S(1)}, bf16[96,2,256]{2,1,0:T(2,128)(2,1)}, u32[]{:S(2)}) copy-start(bf16[96,2,256]{2,1,0:T(2,128)(2,1)} %param.4) | copy-start | bytes 294916
  41.6 48.5 %all-to-all-start.3 = ((bf16[4,8,1,2,128,256]{5,4,3,1,2,0:T(8,128)(2,1)}), bf16[4,8,1,2,128,256]{5,4,3,1,2,0:T(8,128)(2,1)}, u32[]{:S(2)}, u32[]{:S(2)}) async-start(bf16[4,8,1,2,128,256]{5,4,3,1,2,0:T(8,128)(2,1)} %stack.20), calls=%async_computation.3 | async-start | bytes 8388608 | tf_op jit(solution)/shard_map/all_to_all | solution.py:20
  46.5 91.9 %all-gather.2.cloned.1.call-start = ((), (), s32[]{:S(2)}) async-start(), calls=%async_computation.4 | async-start | bytes 2359296 | tf_op jit(solution)/shard_map/all_gather | solution.py:38
Sparse Core Ops, SparseCore 0:
  93.5 44.8 all-gather.1
